TPU v7x, 32 devices: a whole 2x2x4 slice. The times are simulated.
32 devices in a mesh: mode: 8 (over y, x, core), tm: 4 (over z).
Axes of the slice: x: 2, y: 2, z: 4, core: 2. Of those that a mesh axis runs over, the one named last changes fastest.
Arguments:
- field: float32 [2, 128, 65536], P(None, 'mode', 'tm'), may hold values from -1.8 to 1.8
- beta: float32 [3, 128], P(None, 'mode'), may hold values from -1 to 1
- quartets: int32 [4, 1024], replicated, may hold values from 0 to 127
- intersections: float32 [1024], replicated, may hold values from -0.12 to 0.12
Outputs:
- field_out: float32 [2, 128, 65536], P(None, 'mode', 'tm')
- errors: float32 [2, 128], P(None, 'mode')
All inputs are finite; a program needn't handle non-finite values.
Results may differ from a plain program's by a relative error of at most 0.0003.
Values sent between devices are 32-bit elements; how exact they have to be, the bound alone decides.
A program may use at most 128 MiB of HBM per device.

v0:
```python
import math
import jax
import jax.numpy as jnp
from jax import lax
from jax.sharding import PartitionSpec as P

RADIX = 256
STEPS = 2
epsilon = 1e-06


def phase_of(offset, slope, curve, frequency):
    return math.pi * offset + 300.0 * slope * frequency + 3000.0 * curve * frequency * frequency


def triple_product(left_field, middle_field, conj_field):
    prod_re = left_field[0] * middle_field[0] - left_field[1] * middle_field[1]
    prod_im = left_field[0] * middle_field[1] + left_field[1] * middle_field[0]
    out_re = prod_re * conj_field[0] + prod_im * conj_field[1]
    out_im = prod_im * conj_field[0] - prod_re * conj_field[1]
    return (out_re, out_im)


def contract(form, first_operand, second_operand):
    return jnp.einsum(form, first_operand, second_operand, precision=lax.Precision.HIGHEST)


def rotate(real_part, imag_part, angle):
    cosine = jnp.cos(angle)
    sine_part = jnp.sin(angle)
    return (real_part * cosine - imag_part * sine_part, real_part * sine_part + imag_part * cosine)


def dft_tables(length):
    positions = lax.iota(jnp.int32, length)
    product = positions[:, None] * positions[None, :] % length
    angle = -2.0 * math.pi / length * product.astype(jnp.float32)
    return (jnp.cos(angle), jnp.sin(angle))


def to_columns(state):
    return lax.all_to_all(state, "tm", split_axis=3, concat_axis=2, tiled=True)


def to_rows(state):
    return lax.all_to_all(state, "tm", split_axis=2, concat_axis=3, tiled=True)


def linear_step(state, beta, table_re, table_im):
    radix_size = table_re.shape[0]
    total_time = radix_size * radix_size
    cols_local = state.shape[3]
    tm_index = lax.axis_index("tm")
    head_re = contract("ka,mab->mkb", table_re, state[0]) - contract(
        "ka,mab->mkb", table_im, state[1]
    )
    head_im = contract("ka,mab->mkb", table_re, state[1]) + contract(
        "ka,mab->mkb", table_im, state[0]
    )
    column = tm_index * cols_local + lax.iota(jnp.int32, cols_local)
    row_position = lax.iota(jnp.int32, radix_size)
    twist = (
        -2.0
        * math.pi
        / total_time
        * (row_position[:, None] * column[None, :] % total_time).astype(jnp.float32)
    )
    head_re, head_im = rotate(head_re, head_im, twist[None])
    turned = lax.all_to_all(
        jnp.stack([head_re, head_im]), "tm", split_axis=2, concat_axis=3, tiled=True
    )
    spec_re = contract("mcb,kb->mck", turned[0], table_re) - contract(
        "mcb,kb->mck", turned[1], table_im
    )
    spec_im = contract("mcb,kb->mck", turned[1], table_re) + contract(
        "mcb,kb->mck", turned[0], table_im
    )
    rows_local = turned.shape[2]
    first_index = tm_index * rows_local + lax.iota(jnp.int32, rows_local)
    wave = first_index[:, None] + radix_size * row_position[None, :]
    signed = jnp.where(wave < total_time // 2, wave, wave - total_time)
    frequency = signed.astype(jnp.float32) / (total_time / 2)
    angle = phase_of(
        beta[0][:, None, None], beta[1][:, None, None], beta[2][:, None, None], frequency[None]
    )
    spec_re, spec_im = rotate(spec_re, spec_im, angle)
    back_re = contract("mck,kb->mcb", spec_re, table_re) + contract(
        "mck,kb->mcb", spec_im, table_im
    )
    back_im = contract("mck,kb->mcb", spec_im, table_re) - contract(
        "mck,kb->mcb", spec_re, table_im
    )
    untwist = (
        2.0
        * math.pi
        / total_time
        * (first_index[:, None] * row_position[None, :] % total_time).astype(jnp.float32)
    )
    back_re, back_im = rotate(back_re, back_im, untwist[None])
    gathered = lax.all_to_all(
        jnp.stack([back_re, back_im]), "tm", split_axis=3, concat_axis=2, tiled=True
    )
    scale = 1.0 / total_time
    out_re = (
        contract("ka,mkb->mab", table_re, gathered[0])
        + contract("ka,mkb->mab", table_im, gathered[1])
    ) * scale
    out_im = (
        contract("ka,mkb->mab", table_re, gathered[1])
        - contract("ka,mkb->mab", table_im, gathered[0])
    ) * scale
    return jnp.stack([out_re, out_im])


def kerr_term(fields, quartets, intersections):
    count = quartets.shape[1]
    block_size = min(512, count)
    blocks = count // block_size
    grouped = quartets.reshape(4, blocks, block_size).transpose(1, 0, 2)
    weights = intersections.reshape(blocks, block_size)
    modes_all = fields.shape[1]
    mode_ids = lax.iota(jnp.int32, modes_all)

    def accumulate(running, block_item):
        indices, weight = block_item
        out_re, out_im = triple_product(
            jnp.take(fields, indices[1], axis=1),
            jnp.take(fields, indices[2], axis=1),
            jnp.take(fields, indices[3], axis=1),
        )
        owner = (indices[0][None, :] == mode_ids[:, None]).astype(jnp.float32) * weight[None, :]
        add_re = contract("pq,qt->pt", owner, -out_im)
        add_im = contract("pq,qt->pt", owner, out_re)
        return (running + jnp.stack([add_re, add_im]), None)

    running, unused = lax.scan(accumulate, jnp.zeros_like(fields), (grouped, weights))
    return running


def kerr_step(flat, quartets, intersections):
    spread = lax.all_to_all(flat, "mode", split_axis=2, concat_axis=1, tiled=True)
    first = kerr_term(spread, quartets, intersections)
    second = kerr_term(spread + first, quartets, intersections)
    updated = spread + 0.5 * (first + second)
    estimate = 0.5 * (second - first)
    returned, estimate_home = (
        lax.all_to_all(updated, "mode", split_axis=1, concat_axis=2, tiled=True),
        lax.all_to_all(estimate, "mode", split_axis=1, concat_axis=2, tiled=True),
    )
    error_part = jnp.sum(estimate_home * estimate_home, axis=(0, 2))
    field_part = jnp.sum(returned * returned, axis=(0, 2))
    return (returned, error_part, field_part)


def shards(field, beta, quartets, intersections):
    modes_local = field.shape[1]
    time_local = field.shape[2]
    table_re, table_im = dft_tables(RADIX)
    state = field.reshape(2, modes_local, time_local // RADIX, RADIX)
    state = to_columns(state)
    error_rows = []
    for step_index in range(STEPS):
        columns = state
        columns = linear_step(columns, beta, table_re, table_im)
        updated, error_part, field_part = kerr_step(
            columns.reshape(2, modes_local, time_local), quartets, intersections
        )
        error_sq, field_sq = lax.psum((error_part, field_part), "tm")
        error_rows.append(jnp.sqrt(error_sq / (field_sq + epsilon)))
        state = updated.reshape(columns.shape)
    state = to_rows(state)
    errors = jnp.stack(error_rows)
    return (state.reshape(2, modes_local, time_local), errors)


def solution(mesh):
    placed = (P(None, "mode", "tm"), P(None, "mode"), P(), P())
    return jax.shard_map(
        shards,
        mesh=mesh,
        in_specs=placed,
        out_specs=(P(None, "mode", "tm"), P(None, "mode")),
        check_vma=False,
    )
```

profile of v0, /device:TPU:18, one launch (start us, length us, event | category | flops | bytes accessed | tf_op | source)
XLA Modules:
  0.0 1882.4 jit_solution(8491664908036585077)
XLA Ops:
  18.4 44.6 %all-to-all-done = f32[4,1,131072]{2,1,0:T(1,128)S(1)} async-done(((f32[4,1,131072]{2,1,0:T(1,128)}), f32[4,1,131072]{2,1,0:T(1,128)S(1)}, u32[]{:S(2)}, u32[]{:S(2)}) %all-to-all-start) | async-done | bytes 2097184 | tf_op jit(solution)/shard_map/all_to_all | solution.py:42
  133.5 44.1 %all-to-all-done.1 = f32[4,1,131072]{2,1,0:T(1,128)} async-done(((f32[4,1,131072]{2,1,0:T(1,128)}), f32[4,1,131072]{2,1,0:T(1,128)}, u32[]{:S(2)}, u32[]{:S(2)}) %all-to-all-start.1) | async-done | bytes 2097184 | tf_op jit(solution)/shard_map/all_to_all | solution.py:69
  231.1 51.6 %all_to_all.174 = f32[4,1,131072]{2,1,0:T(1,128)} all-to-all(f32[4,1,131072]{2,1,0:T(1,128)S(1)} %reshape.495), channel_id=1, replica_groups=mesh['mode'=8,'tm'=4] {'tm'}, dimensions={0} | all-to-all | bytes 4194304 | tf_op jit(solution)/shard_map/all_to_all | solution.py:100
  337.0 24.7 %reshape.497 = f32[8,1,65536]{2,1,0:T(1,128)} reshape(f32[16384,2,16]{2,1,0:T(2,128)} %bitcast.446) | data formatting | bytes 4194304
  366.8 25.0 %all-to-all-done.3 = f32[8,1,65536]{2,1,0:T(1,128)} async-done(((f32[8,1,65536]{2,1,0:T(1,128)}), f32[8,1,65536]{2,1,0:T(1,128)}, u32[]{:S(2)}, u32[]{:S(2)}) %all-to-all-start.3) | async-done | bytes 2097184 | tf_op jit(solution)/shard_map/all_to_all | solution.py:141
  399.1 28.6 %reshape.498 = f32[16384,2,16]{2,1,0:T(2,128)} reshape(f32[8,65536]{1,0:T(8,128)S(1)} %reduce.13) | data formatting | bytes 4194304
  427.7 21.6 %copy.201 = f32[2,16,8,2048]{3,1,2,0:T(8,128)} copy(f32[2,16,8,2048]{1,0,3,2:T(2,128)} %bitcast.447) | data formatting | bytes 4194304 | tf_op jit(solution)/shard_map/all_to_all | solution.py:141
  452.5 210.8 %while.44 = (s32[]{:T(128)}, f32[2,128,2048]{2,1,0:T(8,128)}, s32[2,4,512]{2,1,0:T(4,128)S(1)}, f32[2,512]{1,0:T(2,128)S(1)}, f32[2,128,2048]{2,0,1:T(2,128)S(1)}, /*index=5*/s32[]{:T(128)}, s32[]{:T(128)}, s32[]{}, s32[]{}, s32[]{}) while((s32[]{:T(128)}, f32[2,128,2048]{2,1,0:T(8,128)}, s32[2,4,512]{2,1,0:T(4,128)S(1)}, ...), condition=%wide.region_1.3_spmd.clone, body=%wide.region_0.2_spmd.clone.sunk | while | flops 3243000320 | bytes 234956048 | solution.py:136
  484.7 19.5 %gather_fusion.1 = f32[512,2,2048]{2,1,0:T(2,128)} fusion(f32[2,128,2048]{2,0,1:T(2,128)S(1)} %get-tuple-element.665, s32[1024]{0:T(1024)S(1)} %pad_clamp_fusion.25), kind=kCustom, calls=%fused_computation.clone.clone.1 | custom fusion | bytes 16779264 | tf_op jit(solution)/shard_map/while/body/eval_jaxpr/jit(_take)/gather | solution.py:127
  517.7 19.7 %gather_fusion.2 = f32[512,2,2048]{2,1,0:T(2,128)} fusion(f32[2,128,2048]{2,0,1:T(2,128)S(1)} %get-tuple-element.665, s32[1024]{0:T(1024)S(1)} %pad_clamp_fusion.26), kind=kCustom, calls=%fused_computation.2.clone.clone.1 | custom fusion | bytes 16779264 | tf_op jit(solution)/shard_map/while/body/eval_jaxpr/jit(_take)/gather | solution.py:129
  588.5 19.8 %gather_fusion.1 = f32[512,2,2048]{2,1,0:T(2,128)} fusion(f32[2,128,2048]{2,0,1:T(2,128)S(1)} %get-tuple-element.665, s32[1024]{0:T(1024)S(1)} %pad_clamp_fusion.25), kind=kCustom, calls=%fused_computation.clone.clone.1 | custom fusion | bytes 16779264 | tf_op jit(solution)/shard_map/while/body/eval_jaxpr/jit(_take)/gather | solution.py:127
  667.4 215.6 %while.45 = (s32[]{:T(128)}, f32[2,128,2048]{2,1,0:T(8,128)}, s32[2,4,512]{2,1,0:T(4,128)S(1)}, f32[2,512]{1,0:T(2,128)S(1)}, f32[2,128,2048]{2,0,1:T(2,128)S(1)}, /*index=5*/s32[]{:T(128)}, s32[]{:T(128)}, s32[]{}, s32[]{}, s32[]{}) while((s32[]{:T(128)}, f32[2,128,2048]{2,1,0:T(8,128)}, s32[2,4,512]{2,1,0:T(4,128)S(1)}, ...), condition=%wide.region_3.5_spmd.clone, body=%wide.region_2.4_spmd.clone.sunk | while | flops 3243000320 | bytes 234956048 | solution.py:136
  702.6 19.8 %gather_fusion.4 = f32[512,2,2048]{2,1,0:T(2,128)} fusion(f32[2,128,2048]{2,0,1:T(2,128)S(1)} %get-tuple-element.695, s32[1024]{0:T(1024)S(1)} %pad_clamp_fusion.28), kind=kCustom, calls=%fused_computation.3.clone.clone.1 | custom fusion | bytes 16779264 | tf_op jit(solution)/shard_map/while/body/eval_jaxpr/jit(_take)/gather | solution.py:127
  806.5 19.5 %gather_fusion.4 = f32[512,2,2048]{2,1,0:T(2,128)} fusion(f32[2,128,2048]{2,0,1:T(2,128)S(1)} %get-tuple-element.695, s32[1024]{0:T(1024)S(1)} %pad_clamp_fusion.28), kind=kCustom, calls=%fused_computation.3.clone.clone.1 | custom fusion | bytes 16779264 | tf_op jit(solution)/shard_map/while/body/eval_jaxpr/jit(_take)/gather | solution.py:127
  839.5 19.7 %gather_fusion.5 = f32[512,2,2048]{2,1,0:T(2,128)} fusion(f32[2,128,2048]{2,0,1:T(2,128)S(1)} %get-tuple-element.695, s32[1024]{0:T(1024)S(1)} %pad_clamp_fusion.29), kind=kCustom, calls=%fused_computation.5.clone.clone.1 | custom fusion | bytes 16779264 | tf_op jit(solution)/shard_map/while/body/eval_jaxpr/jit(_take)/gather | solution.py:129
  889.7 29.1 %all_to_all.175 = f32[2,128,2048]{2,0,1:T(2,128)S(1)} all-to-all(f32[2,128,2048]{2,0,1:T(2,128)S(1)} %copy.171), channel_id=1, replica_groups=mesh['mode'=8,'tm'=4] {'mode'}, dimensions={1} | all-to-all | bytes 4194304 | tf_op jit(solution)/shard_map/all_to_all | solution.py:147
  956.1 51.8 %all_to_all.176 = f32[4,1,131072]{2,1,0:T(1,128)} all-to-all(f32[4,1,131072]{2,1,0:T(1,128)S(1)} %reshape.499), channel_id=1, replica_groups=mesh['mode'=8,'tm'=4] {'tm'}, dimensions={0} | all-to-all | bytes 4194304 | tf_op jit(solution)/shard_map/all_to_all | solution.py:69
  1061.5 51.0 %all_to_all.177 = f32[4,1,131072]{2,1,0:T(1,128)} all-to-all(f32[4,1,131072]{2,1,0:T(1,128)S(1)} %reshape.501), channel_id=1, replica_groups=mesh['mode'=8,'tm'=4] {'tm'}, dimensions={0} | all-to-all | bytes 4194304 | tf_op jit(solution)/shard_map/all_to_all | solution.py:100
  1166.4 24.8 %reshape.503 = f32[8,1,65536]{2,1,0:T(1,128)} reshape(f32[16384,2,16]{2,1,0:T(2,128)} %bitcast.448) | data formatting | bytes 4194304
  1198.9 22.2 %all-to-all-done.7 = f32[8,1,65536]{2,1,0:T(1,128)} async-done(((f32[8,1,65536]{2,1,0:T(1,128)}), f32[8,1,65536]{2,1,0:T(1,128)}, u32[]{:S(2)}, u32[]{:S(2)}) %all-to-all-start.7) | async-done | bytes 2097184 | tf_op jit(solution)/shard_map/all_to_all | solution.py:141
  1234.4 28.7 %reshape.504 = f32[16384,2,16]{2,1,0:T(2,128)} reshape(f32[8,65536]{1,0:T(8,128)S(1)} %reduce.16) | data formatting | bytes 4194304
  1263.1 21.6 %copy.203 = f32[2,16,8,2048]{3,1,2,0:T(8,128)} copy(f32[2,16,8,2048]{1,0,3,2:T(2,128)} %bitcast.449) | data formatting | bytes 4194304 | tf_op jit(solution)/shard_map/all_to_all | solution.py:141
  1288.0 210.6 %while.46 = (s32[]{:T(128)}, f32[2,128,2048]{2,1,0:T(8,128)}, s32[2,4,512]{2,1,0:T(4,128)S(1)}, f32[2,512]{1,0:T(2,128)S(1)}, f32[2,128,2048]{2,0,1:T(2,128)S(1)}, /*index=5*/s32[]{:T(128)}, s32[]{:T(128)}, s32[]{}, s32[]{}, s32[]{}) while((s32[]{:T(128)}, f32[2,128,2048]{2,1,0:T(8,128)}, s32[2,4,512]{2,1,0:T(4,128)S(1)}, ...), condition=%wide.region_5.7_spmd.clone, body=%wide.region_4.6_spmd.clone.sunk | while | flops 3243000320 | bytes 234956048 | solution.py:136
  1320.0 19.8 %gather_fusion.7 = f32[512,2,2048]{2,1,0:T(2,128)} fusion(f32[2,128,2048]{2,0,1:T(2,128)S(1)} %get-tuple-element.725, s32[1024]{0:T(1024)S(1)} %pad_clamp_fusion.31), kind=kCustom, calls=%fused_computation.6.clone.clone.1 | custom fusion | bytes 16779264 | tf_op jit(solution)/shard_map/while/body/eval_jaxpr/jit(_take)/gather | solution.py:127
  1424.0 19.5 %gather_fusion.7 = f32[512,2,2048]{2,1,0:T(2,128)} fusion(f32[2,128,2048]{2,0,1:T(2,128)S(1)} %get-tuple-element.725, s32[1024]{0:T(1024)S(1)} %pad_clamp_fusion.31), kind=kCustom, calls=%fused_computation.6.clone.clone.1 | custom fusion | bytes 16779264 | tf_op jit(solution)/shard_map/while/body/eval_jaxpr/jit(_take)/gather | solution.py:127
  1456.9 19.7 %gather_fusion.8 = f32[512,2,2048]{2,1,0:T(2,128)} fusion(f32[2,128,2048]{2,0,1:T(2,128)S(1)} %get-tuple-element.725, s32[1024]{0:T(1024)S(1)} %pad_clamp_fusion.32), kind=kCustom, calls=%fused_computation.8.clone.clone.1 | custom fusion | bytes 16779264 | tf_op jit(solution)/shard_map/while/body/eval_jaxpr/jit(_take)/gather | solution.py:129
  1502.7 229.3 %while.47 = (s32[]{:T(128)}, f32[2,128,2048]{2,1,0:T(8,128)}, s32[2,4,512]{2,1,0:T(4,128)S(1)}, f32[2,512]{1,0:T(2,128)S(1)}, f32[2,128,2048]{2,0,1:T(2,128)S(1)}, /*index=5*/s32[]{:T(128)}, s32[]{:T(128)}, s32[]{}, s32[]{}, s32[]{}) while((s32[]{:T(128)}, f32[2,128,2048]{2,1,0:T(8,128)}, s32[2,4,512]{2,1,0:T(4,128)S(1)}, ...), condition=%wide.region_7.9_spmd.clone, body=%wide.region_6.8_spmd.clone.sunk | while | flops 3243000320 | bytes 234956048 | solution.py:136
  1538.0 30.0 %gather_fusion.10 = f32[512,2,2048]{2,1,0:T(2,128)} fusion(f32[2,128,2048]{2,0,1:T(2,128)S(1)} %get-tuple-element.755, s32[1024]{0:T(1024)S(1)} %pad_clamp_fusion.34), kind=kCustom, calls=%fused_computation.9.clone.clone.1 | custom fusion | bytes 16779264 | tf_op jit(solution)/shard_map/while/body/eval_jaxpr/jit(_take)/gather | solution.py:127
  1581.4 19.7 %gather_fusion.11 = f32[512,2,2048]{2,1,0:T(2,128)} fusion(f32[2,128,2048]{2,0,1:T(2,128)S(1)} %get-tuple-element.755, s32[1024]{0:T(1024)S(1)} %pad_clamp_fusion.35), kind=kCustom, calls=%fused_computation.11.clone.clone.1 | custom fusion | bytes 16779264 | tf_op jit(solution)/shard_map/while/body/eval_jaxpr/jit(_take)/gather | solution.py:129
  1652.1 19.7 %gather_fusion.10 = f32[512,2,2048]{2,1,0:T(2,128)} fusion(f32[2,128,2048]{2,0,1:T(2,128)S(1)} %get-tuple-element.755, s32[1024]{0:T(1024)S(1)} %pad_clamp_fusion.34), kind=kCustom, calls=%fused_computation.9.clone.clone.1 | custom fusion | bytes 16779264 | tf_op jit(solution)/shard_map/while/body/eval_jaxpr/jit(_take)/gather | solution.py:127
  1748.7 20.6 %all-to-all-done.8 = f32[2,128,2048]{2,0,1:T(2,128)S(1)} async-done(((f32[2,128,2048]{2,0,1:T(2,128)}), f32[2,128,2048]{2,0,1:T(2,128)S(1)}, u32[]{:S(2)}, u32[]{:S(2)}) %all-to-all-start.8) | async-done | bytes 2097184 | tf_op jit(solution)/shard_map/all_to_all | solution.py:147
  1817.5 39.8 %all-reduce = (f32[16]{0:T(128)S(1)}, f32[16]{0:T(128)S(1)}, f32[16]{0:T(128)S(1)}, f32[16]{0:T(128)S(1)}) all-reduce(f32[16]{0:T(128)S(1)} %reduce_sum.56, f32[16]{0:T(128)S(1)} %multiply_reduce_fusion, f32[16]{0:T(128)S(1)} %reduce_sum.52, f32[16]{0:T(128)S(1)} %multiply_reduce_fusion.2), channel_id=1, replica_groups=mesh['mode'=8,'tm'=4] {'tm'}, use_global_device_ids=true, to_apply=%region_15.17 | all-reduce | flops 64 | bytes 512 | tf_op jit(solution)/shard_map/psum | solution.py:168
  (396 shorter events, 1078.4 us)
Async XLA Ops:
  12.9 50.1 %all-to-all-start = ((f32[4,1,131072]{2,1,0:T(1,128)}), f32[4,1,131072]{2,1,0:T(1,128)S(1)}, u32[]{:S(2)}, u32[]{:S(2)}) async-start(f32[4,1,131072]{2,1,0:T(1,128)} %reshape.491), calls=%async_computation | async-start | bytes 4194304 | tf_op jit(solution)/shard_map/all_to_all | solution.py:42
  18.4 86.7 %copy-start.27 = (f32[256,64]{0,1:T(8,128)}, f32[256,64]{0,1:T(8,128)S(1)}, u32[]{:S(2)}) copy-start(f32[256,64]{0,1:T(8,128)S(1)} %get-tuple-element.433) | copy-start | bytes 196612
  18.4 86.7 %copy-start.29 = (f32[256,64]{0,1:T(8,128)}, f32[256,64]{0,1:T(8,128)S(1)}, u32[]{:S(2)}) copy-start(f32[256,64]{0,1:T(8,128)S(1)} %get-tuple-element.434) | copy-start | bytes 196612
  119.9 13.2 copy-start.40
  125.4 52.2 %all-to-all-start.1 = ((f32[4,1,131072]{2,1,0:T(1,128)}), f32[4,1,131072]{2,1,0:T(1,128)}, u32[]{:S(2)}, u32[]{:S(2)}) async-start(f32[4,1,131072]{2,1,0:T(1,128)} %reshape.493), calls=%async_computation.1 | async-start | bytes 4194304 | tf_op jit(solution)/shard_map/all_to_all | solution.py:69
  133.1 74.7 %copy-start.33 = (f32[16]{0:T(128)}, f32[16]{0:T(128)S(1)}, u32[]{:S(2)}) copy-start(f32[16]{0:T(128)S(1)} %get-tuple-element.427) | copy-start | bytes 196
  133.1 74.7 %copy-start.35 = (f32[16]{0:T(128)}, f32[16]{0:T(128)S(1)}, u32[]{:S(2)}) copy-start(f32[16]{0:T(128)S(1)} %get-tuple-element.428) | copy-start | bytes 196
  133.1 74.7 %copy-start.37 = (f32[16]{0:T(128)}, f32[16]{0:T(128)S(1)}, u32[]{:S(2)}) copy-start(f32[16]{0:T(128)S(1)} %get-tuple-element.429) | copy-start | bytes 196
  133.5 74.3 %copy-start.25 = (f32[64,256]{1,0:T(8,128)}, f32[64,256]{1,0:T(8,128)S(1)}, u32[]{:S(2)}) copy-start(f32[64,256]{1,0:T(8,128)S(1)} %get-tuple-element.432) | copy-start | bytes 196612
  133.5 86.2 %copy-start.21 = (f32[64,256]{1,0:T(8,128)}, f32[64,256]{1,0:T(8,128)S(1)}, u32[]{:S(2)}) copy-start(f32[64,256]{1,0:T(8,128)S(1)} %get-tuple-element.430) | copy-start | bytes 196612
  133.5 86.2 %copy-start.23 = (f32[64,256]{1,0:T(8,128)}, f32[64,256]{1,0:T(8,128)S(1)}, u32[]{:S(2)}) copy-start(f32[64,256]{1,0:T(8,128)S(1)} %get-tuple-element.431) | copy-start | bytes 196612
  361.7 30.1 %all-to-all-start.3 = ((f32[8,1,65536]{2,1,0:T(1,128)}), f32[8,1,65536]{2,1,0:T(1,128)}, u32[]{:S(2)}, u32[]{:S(2)}) async-start(f32[8,1,65536]{2,1,0:T(1,128)} %reshape.497), calls=%async_computation.3 | async-start | bytes 4194304 | tf_op jit(solution)/shard_map/all_to_all | solution.py:141
  537.4 9.2 copy-start
  537.5 9.2 copy-start.1
  641.2 9.2 copy-start
  641.2 9.2 copy-start.1
  755.3 9.2 copy-start.2
  755.4 9.2 copy-start.3
  859.2 9.2 copy-start.2
  859.2 9.2 copy-start.3
  930.9 11.7 copy-start.28
  930.9 11.7 copy-start.30
  1191.2 29.9 %all-to-all-start.7 = ((f32[8,1,65536]{2,1,0:T(1,128)}), f32[8,1,65536]{2,1,0:T(1,128)}, u32[]{:S(2)}, u32[]{:S(2)}) async-start(f32[8,1,65536]{2,1,0:T(1,128)} %reshape.503), calls=%async_computation.7 | async-start | bytes 4194304 | tf_op jit(solution)/shard_map/all_to_all | solution.py:141
  1221.1 518.9 %all-to-all-start.10 = ((f32[2,128,2048]{2,0,1:T(2,128)}), f32[2,128,2048]{2,0,1:T(2,128)}, u32[]{:S(2)}, u32[]{:S(2)}) async-start(f32[2,128,2048]{2,0,1:T(2,128)} %copy.193), calls=%async_computation.10 | async-start | bytes 4194304 | tf_op jit(solution)/shard_map/all_to_all | solution.py:148
  1476.6 9.2 copy-start.4
  1476.6 9.2 copy-start.5
  1704.7 9.2 copy-start.6
  1704.7 9.2 copy-start.7
  1739.9 29.3 %all-to-all-start.8 = ((f32[2,128,2048]{2,0,1:T(2,128)}), f32[2,128,2048]{2,0,1:T(2,128)S(1)}, u32[]{:S(2)}, u32[]{:S(2)}) async-start(f32[2,128,2048]{2,0,1:T(2,128)} %copy.188), calls=%async_computation.8 | async-start | bytes 4194304 | tf_op jit(solution)/shard_map/all_to_all | solution.py:147
  1769.3 31.0 %all-to-all-start.11 = ((f32[2,128,2048]{2,0,1:T(2,128)}), f32[2,128,2048]{2,0,1:T(2,128)}, u32[]{:S(2)}, u32[]{:S(2)}) async-start(f32[2,128,2048]{2,0,1:T(2,128)} %copy.194), calls=%async_computation.11 | async-start | bytes 4194304 | tf_op jit(solution)/shard_map/all_to_all | solution.py:148
  1794.5 16.0 copy-start.14
  1800.2 57.6 %all-to-all-start.9 = ((f32[4,1,131072]{2,1,0:T(1,128)}), f32[4,1,131072]{2,1,0:T(1,128)}, u32[]{:S(2)}, u32[]{:S(2)}) async-start(f32[4,1,131072]{2,1,0:T(1,128)} %reshape.505), calls=%async_computation.9 | async-start | bytes 4194304 | tf_op jit(solution)/shard_map/all_to_all | solution.py:46
  (29 other events, 197.8 us)
where the time goes:
time: 1890 us; the launch traced here: 1880 us
  local copies, waits for them, and re-layouts  878 us (46%)
  other arithmetic  397 us (21%)
  blocking collectives  223 us (12%)
  waiting for transfers between devices  162 us (9%)
  matrix products  148 us (8%)
  starting transfers between devices  46.1 us (2%)
  loops' own time  25.8 us (1%)
    unnamed x79, local copies, waits for them, and re-layouts  174 us
    gather x8, local copies, waits for them, and re-layouts, accumulate(): jnp.take(fields, indices[1], axis=1)  168 us
    gather x8, local copies, waits for them, and re-layouts, accumulate(): jnp.take(fields, indices[3], axis=1)  157 us
    gather x8, local copies, waits for them, and re-layouts, accumulate(): jnp.take(fields, indices[2], axis=1)  155 us
    dot_general x44, matrix products, contract(): jnp.einsum(form, first_operand, second_operand, precision=lax.Precision.H...  138 us
    all_to_all x2, blocking collectives, linear_step(): lax.all_to_all(jnp.stack([back_re, back_im]), 'tm', split_axis=3, concat_...  103 us
    select_n x8, other arithmetic, accumulate(): jnp.take(fields, indices[2], axis=1)  99.3 us
    select_n x16, other arithmetic, accumulate(): jnp.take(fields, indices[3], axis=1)  73.6 us
  transfers between devices with their start and end apart: 8, of which 6 were waited for; matrix products, arithmetic and copies ran while one was open for 28% of the time, Pallas kernels for 0%

commit v1 on v0

--- a/solution.py
+++ b/solution.py
@@ -66,9 +66,16 @@
         * (row_position[:, None] * column[None, :] % total_time).astype(jnp.float32)
     )
     head_re, head_im = rotate(head_re, head_im, twist[None])
-    turned = lax.all_to_all(
-        jnp.stack([head_re, head_im]), "tm", split_axis=2, concat_axis=3, tiled=True
+    store_grid = lambda my_data, bus_axis: jnp.concatenate(
+        lax.all_to_all(
+            jnp.stack(jnp.split(my_data, lax.axis_size(bus_axis), axis=2)),
+            axis_name=bus_axis,
+            split_axis=0,
+            concat_axis=0,
+        ),
+        axis=3,
     )
+    turned = store_grid(jnp.stack([head_re, head_im]), bus_axis="tm")
     spec_re = contract("mcb,kb->mck", turned[0], table_re) - contract(
         "mcb,kb->mck", turned[1], table_im
     )

time: 1890 us -> 1910 us (1.011)
  no operation moved by 1% of the time
where the time goes in v1:
time: 1910 us; the launch traced here: 1900 us
  local copies, waits for them, and re-layouts  863 us (45%)
  other arithmetic  403 us (21%)
  blocking collectives  223 us (12%)
  waiting for transfers between devices  162 us (8%)
  matrix products  162 us (8%)
  starting transfers between devices  55.7 us (3%)
  loops' own time  25.8 us (1%)
    unnamed x79, local copies, waits for them, and re-layouts  174 us
    gather x8, local copies, waits for them, and re-layouts, accumulate(): jnp.take(fields, indices[1], axis=1)  168 us
    gather x8, local copies, waits for them, and re-layouts, accumulate(): jnp.take(fields, indices[3], axis=1)  157 us
    gather x8, local copies, waits for them, and re-layouts, accumulate(): jnp.take(fields, indices[2], axis=1)  155 us
    dot_general x44, matrix products, contract(): jnp.einsum(form, first_operand, second_operand, precision=lax.Precision.H...  152 us
    all_to_all x2, blocking collectives, linear_step(): lax.all_to_all(jnp.stack([back_re, back_im]), 'tm', split_axis=3, concat_...  103 us
    select_n x8, other arithmetic, accumulate(): jnp.take(fields, indices[2], axis=1)  99.4 us
    select_n x16, other arithmetic, accumulate(): jnp.take(fields, indices[3], axis=1)  73.6 us
  transfers between devices with their start and end apart: 8, of which 6 were waited for; matrix products, arithmetic and copies ran while one was open for 28% of the time, Pallas kernels for 0%

profile of v1, /device:TPU:18, one launch (start us, length us, event | category | flops | bytes accessed | tf_op | source)
XLA Modules:
  0.0 1896.1 jit_solution(9681170323607881498)
XLA Ops:
  18.4 44.6 %all-to-all-done = f32[4,1,131072]{2,1,0:T(1,128)S(1)} async-done(((f32[4,1,131072]{2,1,0:T(1,128)}), f32[4,1,131072]{2,1,0:T(1,128)S(1)}, u32[]{:S(2)}, u32[]{:S(2)}) %all-to-all-start) | async-done | bytes 2097184 | tf_op jit(solution)/shard_map/all_to_all | solution.py:42
  132.1 44.0 %all-to-all-done.1 = f32[4,1,131072]{2,1,0:T(1,128)} async-done(((f32[4,1,131072]{2,1,0:T(1,128)}), f32[4,1,131072]{2,1,0:T(1,128)}, u32[]{:S(2)}, u32[]{:S(2)}) %all-to-all-start.1) | async-done | bytes 2097184 | tf_op jit(solution)/shard_map/all_to_all | solution.py:70
  231.4 51.7 %all_to_all.154 = f32[4,1,131072]{2,1,0:T(1,128)} all-to-all(f32[4,1,131072]{2,1,0:T(1,128)S(1)} %reshape.505), channel_id=1, replica_groups=mesh['mode'=8,'tm'=4] {'tm'}, dimensions={0} | all-to-all | bytes 4194304 | tf_op jit(solution)/shard_map/all_to_all | solution.py:107
  337.2 24.7 %reshape.507 = f32[8,1,65536]{2,1,0:T(1,128)} reshape(f32[16384,2,16]{2,1,0:T(2,128)} %bitcast.462) | data formatting | bytes 4194304
  367.1 25.0 %all-to-all-done.3 = f32[8,1,65536]{2,1,0:T(1,128)} async-done(((f32[8,1,65536]{2,1,0:T(1,128)}), f32[8,1,65536]{2,1,0:T(1,128)}, u32[]{:S(2)}, u32[]{:S(2)}) %all-to-all-start.3) | async-done | bytes 2097184 | tf_op jit(solution)/shard_map/all_to_all | solution.py:148
  399.3 28.6 %reshape.508 = f32[16384,2,16]{2,1,0:T(2,128)} reshape(f32[8,65536]{1,0:T(8,128)S(1)} %reduce.13) | data formatting | bytes 4194304
  427.9 21.6 %copy.197 = f32[2,16,8,2048]{3,1,2,0:T(8,128)} copy(f32[2,16,8,2048]{1,0,3,2:T(2,128)} %bitcast.463) | data formatting | bytes 4194304 | tf_op jit(solution)/shard_map/all_to_all | solution.py:148
  452.7 211.0 %while.44 = (s32[]{:T(128)}, f32[2,128,2048]{2,1,0:T(8,128)}, s32[2,4,512]{2,1,0:T(4,128)S(1)}, f32[2,512]{1,0:T(2,128)S(1)}, f32[2,128,2048]{2,0,1:T(2,128)S(1)}, /*index=5*/s32[]{:T(128)}, s32[]{:T(128)}, s32[]{}, s32[]{}, s32[]{}) while((s32[]{:T(128)}, f32[2,128,2048]{2,1,0:T(8,128)}, s32[2,4,512]{2,1,0:T(4,128)S(1)}, ...), condition=%wide.region_1.3_spmd.clone, body=%wide.region_0.2_spmd.clone.sunk | while | flops 3243000320 | bytes 234956048 | solution.py:143
  485.0 19.5 %gather_fusion.1 = f32[512,2,2048]{2,1,0:T(2,128)} fusion(f32[2,128,2048]{2,0,1:T(2,128)S(1)} %get-tuple-element.673, s32[1024]{0:T(1024)S(1)} %pad_clamp_fusion.25), kind=kCustom, calls=%fused_computation.clone.clone.1 | custom fusion | bytes 16779264 | tf_op jit(solution)/shard_map/while/body/eval_jaxpr/jit(_take)/gather | solution.py:134
  517.9 19.7 %gather_fusion.2 = f32[512,2,2048]{2,1,0:T(2,128)} fusion(f32[2,128,2048]{2,0,1:T(2,128)S(1)} %get-tuple-element.673, s32[1024]{0:T(1024)S(1)} %pad_clamp_fusion.26), kind=kCustom, calls=%fused_computation.2.clone.clone.1 | custom fusion | bytes 16779264 | tf_op jit(solution)/shard_map/while/body/eval_jaxpr/jit(_take)/gather | solution.py:136
  588.7 19.8 %gather_fusion.1 = f32[512,2,2048]{2,1,0:T(2,128)} fusion(f32[2,128,2048]{2,0,1:T(2,128)S(1)} %get-tuple-element.673, s32[1024]{0:T(1024)S(1)} %pad_clamp_fusion.25), kind=kCustom, calls=%fused_computation.clone.clone.1 | custom fusion | bytes 16779264 | tf_op jit(solution)/shard_map/while/body/eval_jaxpr/jit(_take)/gather | solution.py:134
  622.0 19.5 %gather_fusion.2 = f32[512,2,2048]{2,1,0:T(2,128)} fusion(f32[2,128,2048]{2,0,1:T(2,128)S(1)} %get-tuple-element.673, s32[1024]{0:T(1024)S(1)} %pad_clamp_fusion.26), kind=kCustom, calls=%fused_computation.2.clone.clone.1 | custom fusion | bytes 16779264 | tf_op jit(solution)/shard_map/while/body/eval_jaxpr/jit(_take)/gather | solution.py:136
  667.8 215.6 %while.45 = (s32[]{:T(128)}, f32[2,128,2048]{2,1,0:T(8,128)}, s32[2,4,512]{2,1,0:T(4,128)S(1)}, f32[2,512]{1,0:T(2,128)S(1)}, f32[2,128,2048]{2,0,1:T(2,128)S(1)}, /*index=5*/s32[]{:T(128)}, s32[]{:T(128)}, s32[]{}, s32[]{}, s32[]{}) while((s32[]{:T(128)}, f32[2,128,2048]{2,1,0:T(8,128)}, s32[2,4,512]{2,1,0:T(4,128)S(1)}, ...), condition=%wide.region_3.5_spmd.clone, body=%wide.region_2.4_spmd.clone.sunk | while | flops 3243000320 | bytes 234956048 | solution.py:143
  703.0 19.8 %gather_fusion.4 = f32[512,2,2048]{2,1,0:T(2,128)} fusion(f32[2,128,2048]{2,0,1:T(2,128)S(1)} %get-tuple-element.703, s32[1024]{0:T(1024)S(1)} %pad_clamp_fusion.28), kind=kCustom, calls=%fused_computation.3.clone.clone.1 | custom fusion | bytes 16779264 | tf_op jit(solution)/shard_map/while/body/eval_jaxpr/jit(_take)/gather | solution.py:134
  807.0 19.5 %gather_fusion.4 = f32[512,2,2048]{2,1,0:T(2,128)} fusion(f32[2,128,2048]{2,0,1:T(2,128)S(1)} %get-tuple-element.703, s32[1024]{0:T(1024)S(1)} %pad_clamp_fusion.28), kind=kCustom, calls=%fused_computation.3.clone.clone.1 | custom fusion | bytes 16779264 | tf_op jit(solution)/shard_map/while/body/eval_jaxpr/jit(_take)/gather | solution.py:134
  839.9 19.7 %gather_fusion.5 = f32[512,2,2048]{2,1,0:T(2,128)} fusion(f32[2,128,2048]{2,0,1:T(2,128)S(1)} %get-tuple-element.703, s32[1024]{0:T(1024)S(1)} %pad_clamp_fusion.29), kind=kCustom, calls=%fused_computation.5.clone.clone.1 | custom fusion | bytes 16779264 | tf_op jit(solution)/shard_map/while/body/eval_jaxpr/jit(_take)/gather | solution.py:136
  890.1 29.1 %all_to_all.155 = f32[2,128,2048]{2,0,1:T(2,128)S(1)} all-to-all(f32[2,128,2048]{2,0,1:T(2,128)S(1)} %copy.167), channel_id=1, replica_groups=mesh['mode'=8,'tm'=4] {'mode'}, dimensions={1} | all-to-all | bytes 4194304 | tf_op jit(solution)/shard_map/all_to_all | solution.py:154
  968.1 51.8 %all_to_all.156 = f32[4,1,131072]{2,1,0:T(1,128)} all-to-all(f32[4,1,131072]{2,1,0:T(1,128)S(1)} %reshape.509), channel_id=1, replica_groups=mesh['mode'=8,'tm'=4] {'tm'}, dimensions={0} | all-to-all | bytes 4194304 | tf_op jit(solution)/shard_map/all_to_all | solution.py:70
  1075.2 51.0 %all_to_all.157 = f32[4,1,131072]{2,1,0:T(1,128)} all-to-all(f32[4,1,131072]{2,1,0:T(1,128)S(1)} %reshape.511), channel_id=1, replica_groups=mesh['mode'=8,'tm'=4] {'tm'}, dimensions={0} | all-to-all | bytes 4194304 | tf_op jit(solution)/shard_map/all_to_all | solution.py:107
  1180.1 24.8 %reshape.513 = f32[8,1,65536]{2,1,0:T(1,128)} reshape(f32[16384,2,16]{2,1,0:T(2,128)} %bitcast.464) | data formatting | bytes 4194304
  1212.6 22.2 %all-to-all-done.7 = f32[8,1,65536]{2,1,0:T(1,128)} async-done(((f32[8,1,65536]{2,1,0:T(1,128)}), f32[8,1,65536]{2,1,0:T(1,128)}, u32[]{:S(2)}, u32[]{:S(2)}) %all-to-all-start.7) | async-done | bytes 2097184 | tf_op jit(solution)/shard_map/all_to_all | solution.py:148
  1248.1 28.7 %reshape.514 = f32[16384,2,16]{2,1,0:T(2,128)} reshape(f32[8,65536]{1,0:T(8,128)S(1)} %reduce.16) | data formatting | bytes 4194304
  1276.8 21.6 %copy.199 = f32[2,16,8,2048]{3,1,2,0:T(8,128)} copy(f32[2,16,8,2048]{1,0,3,2:T(2,128)} %bitcast.465) | data formatting | bytes 4194304 | tf_op jit(solution)/shard_map/all_to_all | solution.py:148
  1301.6 210.7 %while.46 = (s32[]{:T(128)}, f32[2,128,2048]{2,1,0:T(8,128)}, s32[2,4,512]{2,1,0:T(4,128)S(1)}, f32[2,512]{1,0:T(2,128)S(1)}, f32[2,128,2048]{2,0,1:T(2,128)S(1)}, /*index=5*/s32[]{:T(128)}, s32[]{:T(128)}, s32[]{}, s32[]{}, s32[]{}) while((s32[]{:T(128)}, f32[2,128,2048]{2,1,0:T(8,128)}, s32[2,4,512]{2,1,0:T(4,128)S(1)}, ...), condition=%wide.region_5.7_spmd.clone, body=%wide.region_4.6_spmd.clone.sunk | while | flops 3243000320 | bytes 234956048 | solution.py:143
  1333.7 19.8 %gather_fusion.7 = f32[512,2,2048]{2,1,0:T(2,128)} fusion(f32[2,128,2048]{2,0,1:T(2,128)S(1)} %get-tuple-element.733, s32[1024]{0:T(1024)S(1)} %pad_clamp_fusion.31), kind=kCustom, calls=%fused_computation.6.clone.clone.1 | custom fusion | bytes 16779264 | tf_op jit(solution)/shard_map/while/body/eval_jaxpr/jit(_take)/gather | solution.py:134
  1470.6 19.7 %gather_fusion.8 = f32[512,2,2048]{2,1,0:T(2,128)} fusion(f32[2,128,2048]{2,0,1:T(2,128)S(1)} %get-tuple-element.733, s32[1024]{0:T(1024)S(1)} %pad_clamp_fusion.32), kind=kCustom, calls=%fused_computation.8.clone.clone.1 | custom fusion | bytes 16779264 | tf_op jit(solution)/shard_map/while/body/eval_jaxpr/jit(_take)/gather | solution.py:136
  1516.4 229.4 %while.47 = (s32[]{:T(128)}, f32[2,128,2048]{2,1,0:T(8,128)}, s32[2,4,512]{2,1,0:T(4,128)S(1)}, f32[2,512]{1,0:T(2,128)S(1)}, f32[2,128,2048]{2,0,1:T(2,128)S(1)}, /*index=5*/s32[]{:T(128)}, s32[]{:T(128)}, s32[]{}, s32[]{}, s32[]{}) while((s32[]{:T(128)}, f32[2,128,2048]{2,1,0:T(8,128)}, s32[2,4,512]{2,1,0:T(4,128)S(1)}, ...), condition=%wide.region_7.9_spmd.clone, body=%wide.region_6.8_spmd.clone.sunk | while | flops 3243000320 | bytes 234956048 | solution.py:143
  1551.7 30.0 %gather_fusion.10 = f32[512,2,2048]{2,1,0:T(2,128)} fusion(f32[2,128,2048]{2,0,1:T(2,128)S(1)} %get-tuple-element.763, s32[1024]{0:T(1024)S(1)} %pad_clamp_fusion.34), kind=kCustom, calls=%fused_computation.9.clone.clone.1 | custom fusion | bytes 16779264 | tf_op jit(solution)/shard_map/while/body/eval_jaxpr/jit(_take)/gather | solution.py:134
  1595.2 19.7 %gather_fusion.11 = f32[512,2,2048]{2,1,0:T(2,128)} fusion(f32[2,128,2048]{2,0,1:T(2,128)S(1)} %get-tuple-element.763, s32[1024]{0:T(1024)S(1)} %pad_clamp_fusion.35), kind=kCustom, calls=%fused_computation.11.clone.clone.1 | custom fusion | bytes 16779264 | tf_op jit(solution)/shard_map/while/body/eval_jaxpr/jit(_take)/gather | solution.py:136
  1665.9 19.7 %gather_fusion.10 = f32[512,2,2048]{2,1,0:T(2,128)} fusion(f32[2,128,2048]{2,0,1:T(2,128)S(1)} %get-tuple-element.763, s32[1024]{0:T(1024)S(1)} %pad_clamp_fusion.34), kind=kCustom, calls=%fused_computation.9.clone.clone.1 | custom fusion | bytes 16779264 | tf_op jit(solution)/shard_map/while/body/eval_jaxpr/jit(_take)/gather | solution.py:134
  1762.5 20.6 %all-to-all-done.8 = f32[2,128,2048]{2,0,1:T(2,128)S(1)} async-done(((f32[2,128,2048]{2,0,1:T(2,128)}), f32[2,128,2048]{2,0,1:T(2,128)S(1)}, u32[]{:S(2)}, u32[]{:S(2)}) %all-to-all-start.8) | async-done | bytes 2097184 | tf_op jit(solution)/shard_map/all_to_all | solution.py:154
  1831.3 39.8 %all-reduce = (f32[16]{0:T(128)S(1)}, f32[16]{0:T(128)S(1)}, f32[16]{0:T(128)S(1)}, f32[16]{0:T(128)S(1)}) all-reduce(f32[16]{0:T(128)S(1)} %reduce_sum.56, f32[16]{0:T(128)S(1)} %multiply_reduce_fusion, f32[16]{0:T(128)S(1)} %reduce_sum.52, f32[16]{0:T(128)S(1)} %multiply_reduce_fusion.2), channel_id=1, replica_groups=mesh['mode'=8,'tm'=4] {'tm'}, use_global_device_ids=true, to_apply=%region_15.17 | all-reduce | flops 64 | bytes 512 | tf_op jit(solution)/shard_map/psum | solution.py:175
  (400 shorter events, 1092.1 us)
Async XLA Ops:
  12.9 50.1 %all-to-all-start = ((f32[4,1,131072]{2,1,0:T(1,128)}), f32[4,1,131072]{2,1,0:T(1,128)S(1)}, u32[]{:S(2)}, u32[]{:S(2)}) async-start(f32[4,1,131072]{2,1,0:T(1,128)} %reshape.501), calls=%async_computation | async-start | bytes 4194304 | tf_op jit(solution)/shard_map/all_to_all | solution.py:42
  18.4 86.6 %copy-start.27 = (f32[256,64]{0,1:T(8,128)}, f32[256,64]{0,1:T(8,128)S(1)}, u32[]{:S(2)}) copy-start(f32[256,64]{0,1:T(8,128)S(1)} %get-tuple-element.441) | copy-start | bytes 196612
  18.4 86.6 %copy-start.29 = (f32[256,64]{0,1:T(8,128)}, f32[256,64]{0,1:T(8,128)S(1)}, u32[]{:S(2)}) copy-start(f32[256,64]{0,1:T(8,128)S(1)} %get-tuple-element.442) | copy-start | bytes 196612
  108.9 22.8 %copy-start.40 = (f32[3,16]{1,0:T(4,128)S(1)}, f32[3,16]{1,0:T(4,128)}, u32[]{:S(2)}) copy-start(f32[3,16]{1,0:T(4,128)} %param.15) | copy-start | bytes 580
  114.4 61.7 %all-to-all-start.1 = ((f32[4,1,131072]{2,1,0:T(1,128)}), f32[4,1,131072]{2,1,0:T(1,128)}, u32[]{:S(2)}, u32[]{:S(2)}) async-start(f32[4,1,131072]{2,1,0:T(1,128)} %reshape.503), calls=%async_computation.1 | async-start | bytes 4194304 | tf_op jit(solution)/shard_map/all_to_all | solution.py:70
  131.7 76.2 %copy-start.33 = (f32[16]{0:T(128)}, f32[16]{0:T(128)S(1)}, u32[]{:S(2)}) copy-start(f32[16]{0:T(128)S(1)} %get-tuple-element.435) | copy-start | bytes 196
  131.7 76.2 %copy-start.35 = (f32[16]{0:T(128)}, f32[16]{0:T(128)S(1)}, u32[]{:S(2)}) copy-start(f32[16]{0:T(128)S(1)} %get-tuple-element.436) | copy-start | bytes 196
  131.7 76.2 %copy-start.37 = (f32[16]{0:T(128)}, f32[16]{0:T(128)S(1)}, u32[]{:S(2)}) copy-start(f32[16]{0:T(128)S(1)} %get-tuple-element.437) | copy-start | bytes 196
  132.1 75.8 %copy-start.25 = (f32[64,256]{1,0:T(8,128)}, f32[64,256]{1,0:T(8,128)S(1)}, u32[]{:S(2)}) copy-start(f32[64,256]{1,0:T(8,128)S(1)} %get-tuple-element.440) | copy-start | bytes 196612
  132.1 87.9 %copy-start.21 = (f32[64,256]{1,0:T(8,128)}, f32[64,256]{1,0:T(8,128)S(1)}, u32[]{:S(2)}) copy-start(f32[64,256]{1,0:T(8,128)S(1)} %get-tuple-element.438) | copy-start | bytes 196612
  132.1 87.9 %copy-start.23 = (f32[64,256]{1,0:T(8,128)}, f32[64,256]{1,0:T(8,128)S(1)}, u32[]{:S(2)}) copy-start(f32[64,256]{1,0:T(8,128)S(1)} %get-tuple-element.439) | copy-start | bytes 196612
  362.0 30.2 %all-to-all-start.3 = ((f32[8,1,65536]{2,1,0:T(1,128)}), f32[8,1,65536]{2,1,0:T(1,128)}, u32[]{:S(2)}, u32[]{:S(2)}) async-start(f32[8,1,65536]{2,1,0:T(1,128)} %reshape.507), calls=%async_computation.3 | async-start | bytes 4194304 | tf_op jit(solution)/shard_map/all_to_all | solution.py:148
  537.7 9.2 copy-start
  537.7 9.2 copy-start.1
  641.5 9.2 copy-start
  641.5 9.2 copy-start.1
  755.7 9.2 copy-start.2
  755.7 9.2 copy-start.3
  859.7 9.2 copy-start.2
  859.7 9.2 copy-start.3
  931.2 24.8 %copy-start.28 = (f32[256,64]{0,1:T(8,128)S(1)}, f32[256,64]{0,1:T(8,128)}, u32[]{:S(2)}) copy-start(f32[256,64]{0,1:T(8,128)} %copy-done.27) | copy-start | bytes 196612
  931.2 24.8 %copy-start.30 = (f32[256,64]{0,1:T(8,128)S(1)}, f32[256,64]{0,1:T(8,128)}, u32[]{:S(2)}) copy-start(f32[256,64]{0,1:T(8,128)} %copy-done.29) | copy-start | bytes 196612
  1204.8 29.9 %all-to-all-start.7 = ((f32[8,1,65536]{2,1,0:T(1,128)}), f32[8,1,65536]{2,1,0:T(1,128)}, u32[]{:S(2)}, u32[]{:S(2)}) async-start(f32[8,1,65536]{2,1,0:T(1,128)} %reshape.513), calls=%async_computation.7 | async-start | bytes 4194304 | tf_op jit(solution)/shard_map/all_to_all | solution.py:148
  1234.8 519.0 %all-to-all-start.10 = ((f32[2,128,2048]{2,0,1:T(2,128)}), f32[2,128,2048]{2,0,1:T(2,128)}, u32[]{:S(2)}, u32[]{:S(2)}) async-start(f32[2,128,2048]{2,0,1:T(2,128)} %copy.189), calls=%async_computation.10 | async-start | bytes 4194304 | tf_op jit(solution)/shard_map/all_to_all | solution.py:155
  1386.4 9.2 copy-start.4
  1386.4 9.2 copy-start.5
  1718.5 9.2 copy-start.6
  1718.5 9.2 copy-start.7
  1753.8 29.3 %all-to-all-start.8 = ((f32[2,128,2048]{2,0,1:T(2,128)}), f32[2,128,2048]{2,0,1:T(2,128)S(1)}, u32[]{:S(2)}, u32[]{:S(2)}) async-start(f32[2,128,2048]{2,0,1:T(2,128)} %copy.184), calls=%async_computation.8 | async-start | bytes 4194304 | tf_op jit(solution)/shard_map/all_to_all | solution.py:154
  1783.1 31.0 %all-to-all-start.11 = ((f32[2,128,2048]{2,0,1:T(2,128)}), f32[2,128,2048]{2,0,1:T(2,128)}, u32[]{:S(2)}, u32[]{:S(2)}) async-start(f32[2,128,2048]{2,0,1:T(2,128)} %copy.190), calls=%async_computation.11 | async-start | bytes 4194304 | tf_op jit(solution)/shard_map/all_to_all | solution.py:155
  1808.3 16.0 copy-start.14
  1814.1 57.6 %all-to-all-start.9 = ((f32[4,1,131072]{2,1,0:T(1,128)}), f32[4,1,131072]{2,1,0:T(1,128)}, u32[]{:S(2)}, u32[]{:S(2)}) async-start(f32[4,1,131072]{2,1,0:T(1,128)} %reshape.515), calls=%async_computation.9 | async-start | bytes 4194304 | tf_op jit(solution)/shard_map/all_to_all | solution.py:46
  (29 other events, 198.0 us)
